TPU v7x, 32 devices: a whole 2x2x4 slice. The times are simulated.
32 devices in a mesh: expert: 4 (over y, core), shard: 8 (over z, x).
Axes of the slice: x: 2, y: 2, z: 4, core: 2. Of those that a mesh axis runs over, the one named last changes fastest.
Arguments:
- master_gate: float32 [128, 2048, 768], P('expert', 'shard'), may hold values from -0.125 to 0.125
- second_gate: bfloat16 [128, 2048, 768], P('expert', 'shard'), may hold values from -0.0625 to 0.0625
- master_up: float32 [128, 2048, 768], P('expert', 'shard'), may hold values from -0.125 to 0.125
- second_up: bfloat16 [128, 2048, 768], P('expert', 'shard'), may hold values from -0.0625 to 0.0625
- router_weight: float32 [2048, 128], P('shard', 'expert'), may hold values from -0.125 to 0.125
- router_gain: float32 [2048], P('shard'), may hold values from 0.25 to 1.75
Outputs:
- final_gate: bfloat16 [128, 768, 2048], P('expert', 'shard')
- final_up: bfloat16 [128, 768, 2048], P('expert', 'shard')
- serve_router: bfloat16 [2048, 128], replicated
All inputs are finite; a program needn't handle non-finite values.
Results may differ from a plain program's by a relative error of at most 0.001.
Values may be sent and summed in bfloat16 or wider, within the bound.
No kernel may reach another device: no remote copies, remote signals or barrier semaphores. Data moves between devices by JAX's collectives and lax.ppermute only.
A program may use at most 192 MiB of HBM per device.

v0:
```python
import jax
import jax.numpy as jnp
from jax import lax
from jax.sharding import PartitionSpec as P


def shards(master_gate, second_gate, master_up, second_up, router_weight, router_gain):
    merged_gate = master_gate + second_gate.astype(jnp.float32)
    merged_up = master_up + second_up.astype(jnp.float32)
    narrow_gate, narrow_up = (merged_gate.astype(jnp.bfloat16), merged_up.astype(jnp.bfloat16))
    final_gate, final_up = (
        lax.all_to_all(narrow_gate, "shard", split_axis=2, concat_axis=1, tiled=True),
        lax.all_to_all(narrow_up, "shard", split_axis=2, concat_axis=1, tiled=True),
    )
    final_gate = jnp.transpose(final_gate, (0, 2, 1))
    final_up = jnp.transpose(final_up, (0, 2, 1))
    part_router = (router_weight * router_gain[:, None]).astype(jnp.bfloat16)
    row_router = lax.all_gather(part_router, "shard", axis=0, tiled=True)
    serve_router = lax.all_gather(row_router, "expert", axis=1, tiled=True)
    return (final_gate, final_up, serve_router)


def solution(mesh):
    in_specs = (
        P("expert", "shard", None),
        P("expert", "shard", None),
        P("expert", "shard", None),
        P("expert", "shard", None),
        P("shard", "expert"),
        P("shard"),
    )
    out_specs = (P("expert", "shard", None), P("expert", "shard", None), P())
    return jax.shard_map(shards, mesh=mesh, in_specs=in_specs, out_specs=out_specs, check_vma=False)
```

profile of v0, /device:TPU:0, one launch (start us, length us, event | category | flops | bytes accessed | tf_op | source)
XLA Modules:
  0.0 713.1 jit_solution(3689968632232905963)
XLA Ops:
  0.6 25.0 %copy.25 = f32[32,256,768]{1,0,2:T(8,128)} copy(f32[32,256,768]{2,1,0:T(8,128)} %param.6) | data formatting | bytes 50331648 | tf_op args[0]
  25.7 16.9 %copy.24 = bf16[32,256,768]{1,0,2:T(8,128)(2,1)} copy(bf16[32,256,768]{2,1,0:T(8,128)(2,1)} %param.7) | data formatting | bytes 25165824 | tf_op args[1]
  42.5 17.3 %add_convert_fusion.1 = bf16[32,256,768]{1,0,2:T(8,128)(2,1)} fusion(f32[32,256,768]{1,0,2:T(8,128)} %copy.25, bf16[32,256,768]{1,0,2:T(8,128)(2,1)} %copy.24), kind=kLoop, calls=%fused_computation.1 | loop fusion | flops 18874368 | bytes 50331648 | tf_op jit(solution)/shard_map/convert_element_type | solution.py:10
  59.8 7.3 %all-to-all-start = ((bf16[32,256,768]{1,0,2:T(8,128)(2,1)}), bf16[32,256,768]{1,0,2:T(8,128)(2,1)}, u32[]{:S(2)}, u32[]{:S(2)}) async-start(bf16[32,256,768]{1,0,2:T(8,128)(2,1)} %add_convert_fusion.1), calls=%async_computation | async-start | bytes 25165824 | tf_op jit(solution)/shard_map/all_to_all | solution.py:12
  67.1 25.0 %copy.29 = f32[32,256,768]{1,0,2:T(8,128)} copy(f32[32,256,768]{2,1,0:T(8,128)} %param.8) | data formatting | bytes 50331648 | tf_op args[2]
  92.2 16.9 %copy.28 = bf16[32,256,768]{1,0,2:T(8,128)(2,1)} copy(bf16[32,256,768]{2,1,0:T(8,128)(2,1)} %param.9) | data formatting | bytes 25165824 | tf_op args[3]
  109.0 17.3 %add_convert_fusion = bf16[32,256,768]{1,0,2:T(8,128)(2,1)} fusion(f32[32,256,768]{1,0,2:T(8,128)} %copy.29, bf16[32,256,768]{1,0,2:T(8,128)(2,1)} %copy.28), kind=kLoop, calls=%fused_computation | loop fusion | flops 18874368 | bytes 50331648 | tf_op jit(solution)/shard_map/convert_element_type | solution.py:10
  126.3 0.0 copy-start
  126.3 0.0 copy-start.1
  126.3 213.9 %all-to-all-done = bf16[32,256,768]{1,0,2:T(8,128)(2,1)} async-done(((bf16[32,256,768]{1,0,2:T(8,128)(2,1)}), bf16[32,256,768]{1,0,2:T(8,128)(2,1)}, u32[]{:S(2)}, u32[]{:S(2)}) %all-to-all-start) | async-done | bytes 12582944 | tf_op jit(solution)/shard_map/all_to_all | solution.py:12
  340.2 5.3 all-to-all-start.1
  345.5 0.0 copy-done
  345.5 0.0 copy-done.1
  345.6 292.2 %all_gather.6 = bf16[2048,32]{0,1:T(8,128)(2,1)S(1)} all-gather(bf16[256,32]{0,1:T(8,128)(2,1)S(1)} %multiply_convert_fusion), channel_id=1, replica_groups=mesh['expert'=4,'shard'=8] {'shard'}, dimensions={0}, use_global_device_ids=true | all-gather | bytes 147456 | tf_op jit(solution)/shard_map/all_gather | solution.py:18
  637.8 7.2 %all_gather.7 = bf16[2048,128]{0,1:T(8,128)(2,1)S(1)} all-gather(bf16[2048,32]{0,1:T(8,128)(2,1)S(1)} %all_gather.6), channel_id=1, replica_groups=mesh['expert'=4,'shard'=8] {'expert'}, dimensions={1}, use_global_device_ids=true | all-gather | bytes 655360 | tf_op jit(solution)/shard_map/all_gather | solution.py:19
  645.0 1.0 copy.32
  646.0 14.1 %copy.27 = bf16[32,8,256,96]{2,1,3,0:T(8,128)(2,1)} copy(bf16[32,8,256,96]{2,0,3,1:T(8,128)(2,1)} %bitcast.2) | data formatting | bytes 25165824 | tf_op jit(solution)/shard_map/all_to_all | solution.py:12
  660.0 19.5 %all_to_all.29 = bf16[32,2048,96]{1,2,0:T(8,128)(2,1)} reshape(bf16[32,8,256,96]{2,1,3,0:T(8,128)(2,1)} %copy.27) | data formatting | bytes 25165824 | tf_op jit(solution)/shard_map/all_to_all | solution.py:12
  679.5 0.0 all-to-all-done.1
  679.5 14.1 %copy.31 = bf16[32,8,256,96]{2,1,3,0:T(8,128)(2,1)} copy(bf16[32,8,256,96]{2,0,3,1:T(8,128)(2,1)} %bitcast.6) | data formatting | bytes 25165824 | tf_op jit(solution)/shard_map/all_to_all | solution.py:13
  693.6 19.5 %all_to_all.33 = bf16[32,2048,96]{1,2,0:T(8,128)(2,1)} reshape(bf16[32,8,256,96]{2,1,3,0:T(8,128)(2,1)} %copy.31) | data formatting | bytes 25165824 | tf_op jit(solution)/shard_map/all_to_all | solution.py:13
  (1 shorter events, 0.0 us)
Async XLA Ops:
  59.8 280.3 %all-to-all-start = ((bf16[32,256,768]{1,0,2:T(8,128)(2,1)}), bf16[32,256,768]{1,0,2:T(8,128)(2,1)}, u32[]{:S(2)}, u32[]{:S(2)}) async-start(bf16[32,256,768]{1,0,2:T(8,128)(2,1)} %add_convert_fusion.1), calls=%async_computation | async-start | bytes 25165824 | tf_op jit(solution)/shard_map/all_to_all | solution.py:12
  126.3 219.2 %copy-start = (f32[256,32]{0,1:T(8,128)S(1)}, f32[256,32]{0,1:T(8,128)}, u32[]{:S(2)}) copy-start(f32[256,32]{0,1:T(8,128)} %param.10) | copy-start | bytes 98308
  126.3 219.2 %copy-start.1 = (f32[256]{0:T(256)S(1)}, f32[256]{0:T(256)}, u32[]{:S(2)}) copy-start(f32[256]{0:T(256)} %param.11) | copy-start | bytes 3076
  340.2 339.3 %all-to-all-start.1 = ((bf16[32,256,768]{1,0,2:T(8,128)(2,1)}), bf16[32,256,768]{1,0,2:T(8,128)(2,1)}, u32[]{:S(2)}, u32[]{:S(2)}) async-start(bf16[32,256,768]{1,0,2:T(8,128)(2,1)} %add_convert_fusion), calls=%async_computation.1 | async-start | bytes 25165824 | tf_op jit(solution)/shard_map/all_to_all | solution.py:13
where the time goes:
time: 716 us; the launch traced here: 713 us
  blocking collectives  299 us (42%)
  waiting for transfers between devices  214 us (30%)
  local copies, waits for them, and re-layouts  152 us (21%)
  other arithmetic  34.6 us (5%)
  starting transfers between devices  12.6 us (2%)
    all_gather x1, blocking collectives, shards(): row_router = lax.all_gather(part_router, 'shard', axis=0, tiled=True)  292 us
    all_to_all x1, waiting for transfers between devices, shards(): lax.all_to_all(narrow_gate, 'shard', split_axis=2, concat_axis=1, tiled=T...  214 us
    unnamed x9, local copies, waits for them, and re-layouts  84.8 us
    all_to_all x2, local copies, waits for them, and re-layouts, shards(): lax.all_to_all(narrow_up, 'shard', split_axis=2, concat_axis=1, tiled=True)  33.6 us
    all_to_all x2, local copies, waits for them, and re-layouts, shards(): lax.all_to_all(narrow_gate, 'shard', split_axis=2, concat_axis=1, tiled=T...  33.5 us
    convert_element_type x1, other arithmetic, shards(): merged_gate.astype(jnp.bfloat16)  17.3 us
    convert_element_type x1, other arithmetic, shards(): merged_up.astype(jnp.bfloat16)  17.3 us
  transfers between devices with their start and end apart: 2, of which 1 were waited for; matrix products, arithmetic and copies ran while one was open for 10% of the time, Pallas kernels for 0%

commit v1 on v0

v1 whole, which is shorter than its diff:
```python
import functools

import jax
import jax.numpy as jnp
from jax import lax
from jax.experimental import pallas as pl
from jax.experimental.pallas import tpu as pltpu
from jax.sharding import PartitionSpec as P


def merge_body(ways, after, me_ref, master_ref, second_ref, *refs):
    parts, whole = refs[after:-1], refs[-1]
    served = whole.shape[0] // ways
    me = me_ref[0]
    for e in range(master_ref.shape[0]):
        merged = master_ref[e] + second_ref[e].astype(jnp.float32)
        whole[...] = merged.astype(jnp.bfloat16).T
        for k in range(ways):
            start = pl.multiple_of((me ^ k) * served, served)
            parts[k][e] = whole[pl.ds(start, served), :]


def merge(ways, me, master, second, first, last, after):
    _, rows, columns = master.shape
    count = last - first
    served = columns // ways
    step = 2 if first % 2 == 0 and count % 2 == 0 else 1
    begin = first // step
    take = pl.BlockSpec((step, rows, columns), lambda i, me: (begin + i, 0, 0))
    give = pl.BlockSpec((step, served, rows), lambda i, me: (i, 0, 0))
    size = count * rows * columns
    return pl.pallas_call(
        functools.partial(merge_body, ways, len(after)),
        grid_spec=pltpu.PrefetchScalarGridSpec(
            num_scalar_prefetch=1,
            grid=(count // step,),
            in_specs=[take, take] + [pl.BlockSpec(memory_space=pl.ANY)] * len(after),
            out_specs=[give] * ways,
            scratch_shapes=[pltpu.VMEM((columns, rows), jnp.bfloat16)],
        ),
        out_shape=[jax.ShapeDtypeStruct((count, served, rows), jnp.bfloat16)] * ways,
        compiler_params=pltpu.CompilerParams(vmem_limit_bytes=60 * 2**20),
        cost_estimate=pl.CostEstimate(flops=20 * size, bytes_accessed=8 * size, transcendentals=0),
        name="merge",
    )(me, master, second, *after)


def place_body(ways, me_ref, *refs):
    parts, out_ref = refs[:ways], refs[-1]
    rows = parts[0].shape[-1]
    me = me_ref[0]
    for k in range(ways):
        start = pl.multiple_of((me ^ k) * rows, rows)
        out_ref[:, :, pl.ds(start, rows)] = parts[k][...]


def place(ways, me, parts, experts, first, out):
    count, served, rows = parts[0].shape
    step = next(s for s in (4, 2, 1) if first % s == 0 and count % s == 0)
    begin = first // step
    take = pl.BlockSpec((step, served, rows), lambda i, me: (i, 0, 0))
    give = pl.BlockSpec((step, served, ways * rows), lambda i, me: (begin + i, 0, 0))
    size = count * served * rows * ways
    held = [] if out is None else [out]
    return pl.pallas_call(
        functools.partial(place_body, ways),
        grid_spec=pltpu.PrefetchScalarGridSpec(
            num_scalar_prefetch=1,
            grid=(count // step,),
            in_specs=[take] * ways + [pl.BlockSpec(memory_space=pl.ANY)] * len(held),
            out_specs=give,
        ),
        out_shape=jax.ShapeDtypeStruct((experts, served, ways * rows), parts[0].dtype),
        input_output_aliases={ways + 1: 0} if held else {},
        compiler_params=pltpu.CompilerParams(vmem_limit_bytes=60 * 2**20),
        cost_estimate=pl.CostEstimate(flops=5 * size, bytes_accessed=4 * size, transcendentals=0),
        name="place",
    )(me, *parts, *held)


def exchange(ways, parts):
    got = [parts[0]] + [None] * (ways - 1)
    for k in reversed(range(1, ways)):
        got[k] = lax.ppermute(parts[k], "shard", [(i, i ^ k) for i in range(ways)])
    return got


def gather_router(part_router):
    row_router = lax.all_gather(part_router, "shard", axis=0, tiled=True)
    return lax.all_gather(row_router, "expert", axis=1, tiled=True)


def plain(master, second):
    merged = (master + second.astype(jnp.float32)).astype(jnp.bfloat16)
    final = lax.all_to_all(merged, "shard", split_axis=2, concat_axis=1, tiled=True)
    return jnp.transpose(final, (0, 2, 1))


def usable(ways, experts, rows, columns):
    return rows % 128 == 0 and columns % (16 * ways) == 0 and ways & (ways - 1) == 0 and experts >= 8


def shards(ways, master_gate, second_gate, master_up, second_up, router_weight, router_gain):
    experts, rows, columns = master_gate.shape
    part_router = (router_weight * router_gain[:, None]).astype(jnp.bfloat16)
    if not usable(ways, experts, rows, columns):
        return plain(master_gate, second_gate), plain(master_up, second_up), gather_router(part_router)
    return regroup(ways, master_gate, second_gate, master_up, second_up, part_router)


def regroup(ways, master_gate, second_gate, master_up, second_up, part_router):
    experts = master_gate.shape[0]
    me = lax.axis_index("shard").astype(jnp.int32)[None]
    few = experts // 8
    gate_cuts = ((0, few), (few, experts))
    up_cuts = ((0, experts - few), (experts - few, experts))
    router_parts = exchange(ways, [part_router.T[None]] * ways)
    sides = ((master_gate, second_gate, gate_cuts), (master_up, second_up, up_cuts))
    came, after, turn = [], [], 0
    for master, second, cuts in sides:
        pieces = []
        for first, last in cuts:
            parts = merge(ways, me, master, second, first, last, after)
            after = [parts[0]]
            pieces.append((first, exchange(ways, parts)))
            turn += 1
        came.append(pieces)
    finals = []
    for pieces in came:
        out = None
        for first, parts in pieces:
            out = place(ways, me, parts, experts, first, out)
        finals.append(out)
    row_router = place(ways, me, router_parts, 1, 0, None)[0]
    serve_router = lax.all_gather(row_router, "expert", axis=0, tiled=True).T
    return finals[0], finals[1], serve_router


def solution(mesh):
    in_specs = (
        P("expert", "shard", None),
        P("expert", "shard", None),
        P("expert", "shard", None),
        P("expert", "shard", None),
        P("shard", "expert"),
        P("shard"),
    )
    out_specs = (P("expert", "shard", None), P("expert", "shard", None), P())
    ways = mesh.shape["shard"]
    return jax.shard_map(
        functools.partial(shards, ways), mesh=mesh, in_specs=in_specs, out_specs=out_specs, check_vma=False
    )
```

time: 716 us -> 662 us (0.925)
  the two profiles are of different devices: /device:TPU:0 before, /device:TPU:19 now
where the time goes in v1:
time: 662 us; the launch traced here: 661 us
  waiting for transfers between devices  529 us (80%)
  Pallas kernels  73.9 us (11%)
  starting transfers between devices  45.6 us (7%)
  blocking collectives  10.5 us (2%)
    ppermute x35, waiting for transfers between devices, exchange(): got[k] = lax.ppermute(parts[k], 'shard', [(i, i ^ k) for i in range(ways)])  529 us
    ppermute x35, starting transfers between devices, exchange(): got[k] = lax.ppermute(parts[k], 'shard', [(i, i ^ k) for i in range(ways)])  45.6 us
    pallas_call x4, Pallas kernels, merge(): pl.pallas_call(functools.partial(merge_body, ways, len(after)), grid_spec...  44.6 us
    pallas_call x5, Pallas kernels, place(): pl.pallas_call(functools.partial(place_body, ways), grid_spec=pltpu.Prefe...  29.3 us
  transfers between devices with their start and end apart: 35, of which 14 were waited for; matrix products, arithmetic and copies ran while one was open for 0% of the time, Pallas kernels for 10%

profile of v1, /device:TPU:19, one launch (start us, length us, event | category | flops | bytes accessed | tf_op | source)
XLA Modules:
  0.0 661.1 jit_solution(10464251641201522269)
XLA Ops:
  0.7 3.5 merge.4
  4.2 0.3 collective-permute-start.7
  4.4 1.3 collective-permute-start.8
  5.8 1.3 collective-permute-start.28
  7.2 1.3 collective-permute-start.30
  8.5 2.1 collective-permute-done.28.refs_1_
  10.6 2.3 collective-permute-start.32
  12.9 1.0 collective-permute-start.33
  14.0 1.3 collective-permute-start.34
  15.3 3.1 collective-permute-start.9
  18.4 18.8 %merge.5 = (bf16[28,96,256]{2,1,0:T(8,128)(2,1)}, bf16[28,96,256]{2,1,0:T(8,128)(2,1)}, bf16[28,96,256]{2,1,0:T(8,128)(2,1)}, bf16[28,96,256]{2,1,0:T(8,128)(2,1...) custom-call(s32[1]{0:T(128)} %bitcast.me_ref, ...), custom_call_target="tpu_custom_call" | custom-call | flops 110100480 | bytes 44040192 | tf_op jit(solution)/shard_map/merge/pallas_call | solution.py:32
  37.3 1.3 collective-permute-start
  38.6 1.4 collective-permute-start.2
  40.3 2.1 collective-permute-start.10
  42.4 86.6 %collective-permute-done.10.refs_4_ = bf16[4,96,256]{2,1,0:T(8,128)(2,1)S(1)} collective-permute-done((bf16[4,96,256]{2,1,0:T(8,128)(2,1)S(1)}, bf16[4,96,256]{2,1,0:T(8,128)(2,1)S(1)}, u32[]{:S(2)}, u32[]{:S(2)}) %collective-permute-start.10) | collective-permute-done | bytes 196640 | tf_op jit(solution)/shard_map/ppermute | solution.py:84
  129.2 12.3 %collective-permute-done.11.refs_5_ = bf16[4,96,256]{2,1,0:T(8,128)(2,1)S(1)} collective-permute-done((bf16[4,96,256]{2,1,0:T(8,128)(2,1)}, bf16[4,96,256]{2,1,0:T(8,128)(2,1)S(1)}, u32[]{:S(2)}, u32[]{:S(2)}) %collective-permute-start.11) | collective-permute-done | bytes 196640 | tf_op jit(solution)/shard_map/ppermute | solution.py:84
  141.6 10.2 %collective-permute-done.12.refs_6_ = bf16[4,96,256]{2,1,0:T(8,128)(2,1)} collective-permute-done((bf16[4,96,256]{2,1,0:T(8,128)(2,1)S(1)}, bf16[4,96,256]{2,1,0:T(8,128)(2,1)}, u32[]{:S(2)}, u32[]{:S(2)}) %collective-permute-start.12) | collective-permute-done | bytes 196640 | tf_op jit(solution)/shard_map/ppermute | solution.py:84
  151.8 18.8 %merge.6 = (bf16[28,96,256]{2,1,0:T(8,128)(2,1)}, bf16[28,96,256]{2,1,0:T(8,128)(2,1)}, bf16[28,96,256]{2,1,0:T(8,128)(2,1)}, bf16[28,96,256]{2,1,0:T(8,128)(2,1...) custom-call(s32[1]{0:T(128)} %bitcast.me_ref, ...), custom_call_target="tpu_custom_call" | custom-call | flops 110100480 | bytes 44040192 | tf_op jit(solution)/shard_map/merge/pallas_call | solution.py:32
  170.7 3.5 merge.7
  174.2 0.7 copy-done.9
  174.9 1.3 collective-permute-start.14
  176.2 4.2 collective-permute-done.14.refs_1_
  180.4 2.2 collective-permute-start.15
  182.6 3.3 collective-permute-done.15.refs_2_
  185.9 1.7 collective-permute-start.4
  187.6 1.0 collective-permute-start.5
  188.6 1.0 collective-permute-start.6
  189.6 0.8 collective-permute-start.21
  190.3 3.6 collective-permute-start.22
  193.9 110.9 %collective-permute-done.4.refs_5_ = bf16[28,96,256]{2,1,0:T(8,128)(2,1)} collective-permute-done((bf16[28,96,256]{2,1,0:T(8,128)(2,1)}, bf16[28,96,256]{2,1,0:T(8,128)(2,1)}, u32[]{:S(2)}, u32[]{:S(2)}) %collective-permute-start.4) | collective-permute-done | bytes 1376288 | tf_op jit(solution)/shard_map/ppermute | solution.py:84
  304.8 5.0 collective-permute-start.23
  309.8 27.4 %collective-permute-done.5.refs_6_ = bf16[28,96,256]{2,1,0:T(8,128)(2,1)} collective-permute-done((bf16[28,96,256]{2,1,0:T(8,128)(2,1)}, bf16[28,96,256]{2,1,0:T(8,128)(2,1)}, u32[]{:S(2)}, u32[]{:S(2)}) %collective-permute-start.5) | collective-permute-done | bytes 1376288 | tf_op jit(solution)/shard_map/ppermute | solution.py:84
  337.2 61.3 %collective-permute-done.6.refs_7_ = bf16[28,96,256]{2,1,0:T(8,128)(2,1)} collective-permute-done((bf16[28,96,256]{2,1,0:T(8,128)(2,1)}, bf16[28,96,256]{2,1,0:T(8,128)(2,1)}, u32[]{:S(2)}, u32[]{:S(2)}) %collective-permute-start.6) | collective-permute-done | bytes 1376288 | tf_op jit(solution)/shard_map/ppermute | solution.py:84
  398.5 1.5 collective-permute-start.27
  400.0 1.5 place.9
  401.5 3.1 collective-permute-start.16
  404.7 108.0 %collective-permute-done.24.refs_4_ = bf16[28,96,256]{2,1,0:T(8,128)(2,1)} collective-permute-done((bf16[28,96,256]{2,1,0:T(8,128)(2,1)}, bf16[28,96,256]{2,1,0:T(8,128)(2,1)}, u32[]{:S(2)}, u32[]{:S(2)}) %collective-permute-start.24) | collective-permute-done | bytes 1376288 | tf_op jit(solution)/shard_map/ppermute | solution.py:84
  512.7 3.1 collective-permute-start.17
  515.8 30.6 %collective-permute-done.25.refs_5_ = bf16[28,96,256]{2,1,0:T(8,128)(2,1)} collective-permute-done((bf16[28,96,256]{2,1,0:T(8,128)(2,1)}, bf16[28,96,256]{2,1,0:T(8,128)(2,1)}, u32[]{:S(2)}, u32[]{:S(2)}) %collective-permute-start.25) | collective-permute-done | bytes 1376288 | tf_op jit(solution)/shard_map/ppermute | solution.py:84
  546.4 4.0 collective-permute-start.18
  550.4 41.1 %collective-permute-done.26.refs_6_ = bf16[28,96,256]{2,1,0:T(8,128)(2,1)} collective-permute-done((bf16[28,96,256]{2,1,0:T(8,128)(2,1)}, bf16[28,96,256]{2,1,0:T(8,128)(2,1)}, u32[]{:S(2)}, u32[]{:S(2)}) %collective-permute-start.26) | collective-permute-done | bytes 1376288 | tf_op jit(solution)/shard_map/ppermute | solution.py:84
  591.5 30.4 %collective-permute-done.27.refs_7_ = bf16[28,96,256]{2,1,0:T(8,128)(2,1)} collective-permute-done((bf16[28,96,256]{2,1,0:T(8,128)(2,1)}, bf16[28,96,256]{2,1,0:T(8,128)(2,1)}, u32[]{:S(2)}, u32[]{:S(2)}) %collective-permute-start.27) | collective-permute-done | bytes 1376288 | tf_op jit(solution)/shard_map/ppermute | solution.py:84
  621.8 10.5 %all-gather = bf16[1,128,2048]{2,1,0:T(8,128)(2,1)S(1)} all-gather(bf16[1,32,2048]{2,1,0:T(8,128)(2,1)} %place.9), channel_id=2, replica_groups=mesh['expert'=4,'shard'=8] {'expert'}, dimensions={1}, use_global_device_ids=true | all-gather | bytes 655360 | tf_op jit(solution)/shard_map/all_gather | solution.py:135
  632.3 1.0 copy.11
  633.3 2.8 place.5.refs_8_
  636.1 11.1 %place.7.refs_8_ = bf16[32,96,2048]{2,1,0:T(8,128)(2,1)} custom-call(s32[1]{0:T(128)} %bitcast.me_ref, bf16[28,96,256]{2,1,0:T(8,128)(2,1)} %get-tuple-element.51.refs_0_, bf16[28,96,256]{2,1,0:T(8,128)(2,1)} %collective-permute-done.21.refs_1_, bf16[28,96,256]{2,1,0:T(8,128)(2,1)} %collective-permute-done.22.refs_2_, ...), custom_call_target="tpu_custom_call" | custom-call | flops 27525120 | bytes 22020096 | tf_op jit(solution)/shard_map/place/pallas_call | solution.py:65
  647.2 11.1 %place.6 = bf16[32,96,2048]{2,1,0:T(8,128)(2,1)} custom-call(s32[1]{0:T(128)} %bitcast.me_ref, bf16[28,96,256]{2,1,0:T(8,128)(2,1)} %get-tuple-element.36.refs_0_, bf16[28,96,256]{2,1,0:T(8,128)(2,1)} %copy-done, bf16[28,96,256]{2,1,0:T(8,128)(2,1)} %copy-done.1, ...), custom_call_target="tpu_custom_call", output_to_operand_aliasing={{}: (9, {})} | custom-call | flops 27525120 | bytes 22020096 | tf_op jit(solution)/shard_map/place/pallas_call | solution.py:65
  658.3 2.8 place.8
  (78 shorter events, 1.0 us)
Async XLA Ops:
  4.2 34.4 %collective-permute-start.7 = (bf16[4,96,256]{2,1,0:T(8,128)(2,1)}, bf16[4,96,256]{2,1,0:T(8,128)(2,1)S(1)}, u32[]{:S(2)}, u32[]{:S(2)}) collective-permute-start(bf16[4,96,256]{2,1,0:T(8,128)(2,1)} %get-tuple-element.44), channel_id=1, source_target_pairs={{0,1},{1,0},{2,3},{3,2},{4,5},{5,4},{6,7},{7,6},{8,9},{9,8},{10,11... | collective-permute-start | bytes 589832 | tf_op jit(solution)/shard_map/ppermute | solution.py:84
  4.4 35.5 %collective-permute-start.8 = (bf16[4,96,256]{2,1,0:T(8,128)(2,1)}, bf16[4,96,256]{2,1,0:T(8,128)(2,1)S(1)}, u32[]{:S(2)}, u32[]{:S(2)}) collective-permute-start(bf16[4,96,256]{2,1,0:T(8,128)(2,1)} %get-tuple-element.45), channel_id=1, source_target_pairs={{0,2},{1,3},{2,0},{3,1},{4,6},{5,7},{6,4},{7,5},{8,10},{9,11},{10,... | collective-permute-start | bytes 589832 | tf_op jit(solution)/shard_map/ppermute | solution.py:84
  5.8 31.4 %copy-start.10 = (bf16[1,32,256]{2,1,0:T(8,128)(2,1)}, bf16[1,32,256]{2,1,0:T(8,128)(2,1)S(1)}, u32[]{:S(2)}) copy-start(bf16[1,32,256]{2,1,0:T(8,128)(2,1)S(1)} %fusion.refs_0_) | copy-start | bytes 49156
  5.8 4.8 collective-permute-start.28
  7.0 3.6 collective-permute-start.29
  7.2 5.7 collective-permute-start.30
  10.5 26.6 %copy-start.12 = (bf16[1,32,256]{2,1,0:T(8,128)(2,1)}, bf16[1,32,256]{2,1,0:T(8,128)(2,1)S(1)}, u32[]{:S(2)}) copy-start(bf16[1,32,256]{2,1,0:T(8,128)(2,1)S(1)} %collective-permute-done.28.refs_1_) | copy-start | bytes 49156
  10.5 3.5 collective-permute-start.31
  10.6 4.7 collective-permute-start.32
  12.9 24.3 %collective-permute-start.33 = (bf16[1,32,256]{2,1,0:T(8,128)(2,1)S(1)}, bf16[1,32,256]{2,1,0:T(8,128)(2,1)S(1)}, u32[]{:S(2)}, u32[]{:S(2)}) collective-permute-start(bf16[1,32,256]{2,1,0:T(8,128)(2,1)S(1)} %fusion.refs_0_), channel_id=1, source_target_pairs={{0,6},{1,7},{2,4},{3,5},{4,2},{5,3},{6,0},{7,1},{8,14},{9,15},{10,... | collective-permute-start | bytes 49160 | tf_op jit(solution)/shard_map/ppermute | solution.py:84
  14.0 24.5 %collective-permute-start.34 = (bf16[1,32,256]{2,1,0:T(8,128)(2,1)S(1)}, bf16[1,32,256]{2,1,0:T(8,128)(2,1)S(1)}, u32[]{:S(2)}, u32[]{:S(2)}) collective-permute-start(bf16[1,32,256]{2,1,0:T(8,128)(2,1)S(1)} %fusion.refs_0_), channel_id=1, source_target_pairs={{0,7},{1,6},{2,5},{3,4},{4,3},{5,2},{6,1},{7,0},{8,15},{9,14},{10,... | collective-permute-start | bytes 49160 | tf_op jit(solution)/shard_map/ppermute | solution.py:84
  15.3 25.0 %collective-permute-start.9 = (bf16[4,96,256]{2,1,0:T(8,128)(2,1)}, bf16[4,96,256]{2,1,0:T(8,128)(2,1)S(1)}, u32[]{:S(2)}, u32[]{:S(2)}) collective-permute-start(bf16[4,96,256]{2,1,0:T(8,128)(2,1)} %get-tuple-element.46), channel_id=1, source_target_pairs={{0,3},{1,2},{2,1},{3,0},{4,7},{5,6},{6,5},{7,4},{8,11},{9,10},{10,... | collective-permute-start | bytes 589832 | tf_op jit(solution)/shard_map/ppermute | solution.py:84
  18.4 123.2 %copy-start.20 = (bf16[4,96,256]{2,1,0:T(8,128)(2,1)S(1)}, bf16[4,96,256]{2,1,0:T(8,128)(2,1)}, u32[]{:S(2)}) copy-start(bf16[4,96,256]{2,1,0:T(8,128)(2,1)} %get-tuple-element.49) | copy-start | bytes 589828
  37.2 133.4 %copy-start.17 = (bf16[1,32,256]{2,1,0:T(8,128)(2,1)}, bf16[1,32,256]{2,1,0:T(8,128)(2,1)S(1)}, u32[]{:S(2)}) copy-start(bf16[1,32,256]{2,1,0:T(8,128)(2,1)S(1)} %collective-permute-done.33.refs_6_) | copy-start | bytes 49156
  37.3 150.3 %collective-permute-start = (bf16[28,96,256]{2,1,0:T(8,128)(2,1)}, bf16[28,96,256]{2,1,0:T(8,128)(2,1)S(1)}, u32[]{:S(2)}, u32[]{:S(2)}) collective-permute-start(bf16[28,96,256]{2,1,0:T(8,128)(2,1)} %get-tuple-element.37), channel_id=1, source_target_pairs={{0,1},{1,0},{2,3},{3,2},{4,5},{5,4},{6,7},{7,6},{8,9},{9,8},{10,11... | collective-permute-start | bytes 4128776 | tf_op jit(solution)/shard_map/ppermute | solution.py:84
  38.5 132.1 %copy-start.18 = (bf16[1,32,256]{2,1,0:T(8,128)(2,1)}, bf16[1,32,256]{2,1,0:T(8,128)(2,1)S(1)}, u32[]{:S(2)}) copy-start(bf16[1,32,256]{2,1,0:T(8,128)(2,1)S(1)} %collective-permute-done.34.refs_7_) | copy-start | bytes 49156
  38.5 150.0 %collective-permute-start.1 = (bf16[28,96,256]{2,1,0:T(8,128)(2,1)}, bf16[28,96,256]{2,1,0:T(8,128)(2,1)S(1)}, u32[]{:S(2)}, u32[]{:S(2)}) collective-permute-start(bf16[28,96,256]{2,1,0:T(8,128)(2,1)} %get-tuple-element.38), channel_id=1, source_target_pairs={{0,2},{1,3},{2,0},{3,1},{4,6},{5,7},{6,4},{7,5},{8,10},{9,11},{10,... | collective-permute-start | bytes 4128776 | tf_op jit(solution)/shard_map/ppermute | solution.py:84
  38.6 132.1 %copy-start.4 = (bf16[4,96,256]{2,1,0:T(8,128)(2,1)}, bf16[4,96,256]{2,1,0:T(8,128)(2,1)S(1)}, u32[]{:S(2)}) copy-start(bf16[4,96,256]{2,1,0:T(8,128)(2,1)S(1)} %collective-permute-done.7.refs_1_) | copy-start | bytes 589828
  38.6 151.0 %collective-permute-start.2 = (bf16[28,96,256]{2,1,0:T(8,128)(2,1)}, bf16[28,96,256]{2,1,0:T(8,128)(2,1)}, u32[]{:S(2)}, u32[]{:S(2)}) collective-permute-start(bf16[28,96,256]{2,1,0:T(8,128)(2,1)} %get-tuple-element.39), channel_id=1, source_target_pairs={{0,3},{1,2},{2,1},{3,0},{4,7},{5,6},{6,5},{7,4},{8,11},{9,10},{10,... | collective-permute-start | bytes 4128776 | tf_op jit(solution)/shard_map/ppermute | solution.py:84
  40.0 130.7 %copy-start.5 = (bf16[4,96,256]{2,1,0:T(8,128)(2,1)}, bf16[4,96,256]{2,1,0:T(8,128)(2,1)S(1)}, u32[]{:S(2)}) copy-start(bf16[4,96,256]{2,1,0:T(8,128)(2,1)S(1)} %collective-permute-done.8.refs_2_) | copy-start | bytes 589828
  40.0 150.3 %collective-permute-start.3 = (bf16[28,96,256]{2,1,0:T(8,128)(2,1)}, bf16[28,96,256]{2,1,0:T(8,128)(2,1)}, u32[]{:S(2)}, u32[]{:S(2)}) collective-permute-start(bf16[28,96,256]{2,1,0:T(8,128)(2,1)} %get-tuple-element.40), channel_id=1, source_target_pairs={{0,4},{1,5},{2,6},{3,7},{4,0},{5,1},{6,2},{7,3},{8,12},{9,13},{10,... | collective-permute-start | bytes 4128776 | tf_op jit(solution)/shard_map/ppermute | solution.py:84
  40.3 130.4 %copy-start.6 = (bf16[4,96,256]{2,1,0:T(8,128)(2,1)}, bf16[4,96,256]{2,1,0:T(8,128)(2,1)S(1)}, u32[]{:S(2)}) copy-start(bf16[4,96,256]{2,1,0:T(8,128)(2,1)S(1)} %collective-permute-done.9.refs_3_) | copy-start | bytes 589828
  40.3 88.8 %collective-permute-start.10 = (bf16[4,96,256]{2,1,0:T(8,128)(2,1)S(1)}, bf16[4,96,256]{2,1,0:T(8,128)(2,1)S(1)}, u32[]{:S(2)}, u32[]{:S(2)}) collective-permute-start(bf16[4,96,256]{2,1,0:T(8,128)(2,1)S(1)} %copy-done.21), channel_id=1, source_target_pairs={{0,4},{1,5},{2,6},{3,7},{4,0},{5,1},{6,2},{7,3},{8,12},{9,13},{10,... | collective-permute-start | bytes 589832 | tf_op jit(solution)/shard_map/ppermute | solution.py:84
  129.0 41.7 %copy-start.7 = (bf16[4,96,256]{2,1,0:T(8,128)(2,1)}, bf16[4,96,256]{2,1,0:T(8,128)(2,1)S(1)}, u32[]{:S(2)}) copy-start(bf16[4,96,256]{2,1,0:T(8,128)(2,1)S(1)} %collective-permute-done.10.refs_4_) | copy-start | bytes 589828
  129.0 12.5 %collective-permute-start.11 = (bf16[4,96,256]{2,1,0:T(8,128)(2,1)}, bf16[4,96,256]{2,1,0:T(8,128)(2,1)S(1)}, u32[]{:S(2)}, u32[]{:S(2)}) collective-permute-start(bf16[4,96,256]{2,1,0:T(8,128)(2,1)} %get-tuple-element.48), channel_id=1, source_target_pairs={{0,5},{1,4},{2,7},{3,6},{4,1},{5,0},{6,3},{7,2},{8,13},{9,12},{10,... | collective-permute-start | bytes 589832 | tf_op jit(solution)/shard_map/ppermute | solution.py:84
  141.6 29.1 %copy-start.8 = (bf16[4,96,256]{2,1,0:T(8,128)(2,1)}, bf16[4,96,256]{2,1,0:T(8,128)(2,1)S(1)}, u32[]{:S(2)}) copy-start(bf16[4,96,256]{2,1,0:T(8,128)(2,1)S(1)} %collective-permute-done.11.refs_5_) | copy-start | bytes 589828
  141.6 10.2 %collective-permute-start.12 = (bf16[4,96,256]{2,1,0:T(8,128)(2,1)S(1)}, bf16[4,96,256]{2,1,0:T(8,128)(2,1)}, u32[]{:S(2)}, u32[]{:S(2)}) collective-permute-start(bf16[4,96,256]{2,1,0:T(8,128)(2,1)S(1)} %copy-done.20), channel_id=1, source_target_pairs={{0,6},{1,7},{2,4},{3,5},{4,2},{5,3},{6,0},{7,1},{8,14},{9,15},{10,... | collective-permute-start | bytes 589832 | tf_op jit(solution)/shard_map/ppermute | solution.py:84
  151.8 22.4 %collective-permute-start.13 = (bf16[4,96,256]{2,1,0:T(8,128)(2,1)}, bf16[4,96,256]{2,1,0:T(8,128)(2,1)S(1)}, u32[]{:S(2)}, u32[]{:S(2)}) collective-permute-start(bf16[4,96,256]{2,1,0:T(8,128)(2,1)} %get-tuple-element.50), channel_id=1, source_target_pairs={{0,7},{1,6},{2,5},{3,4},{4,3},{5,2},{6,1},{7,0},{8,15},{9,14},{10,... | collective-permute-start | bytes 589832 | tf_op jit(solution)/shard_map/ppermute | solution.py:84
  174.9 5.6 collective-permute-start.14
  180.4 455.7 %copy-start.2 = (bf16[4,96,256]{2,1,0:T(8,128)(2,1)}, bf16[4,96,256]{2,1,0:T(8,128)(2,1)S(1)}, u32[]{:S(2)}) copy-start(bf16[4,96,256]{2,1,0:T(8,128)(2,1)S(1)} %collective-permute-done.14.refs_1_) | copy-start | bytes 589828
  180.4 5.5 collective-permute-start.15
  185.9 118.9 %collective-permute-start.4 = (bf16[28,96,256]{2,1,0:T(8,128)(2,1)}, bf16[28,96,256]{2,1,0:T(8,128)(2,1)}, u32[]{:S(2)}, u32[]{:S(2)}) collective-permute-start(bf16[28,96,256]{2,1,0:T(8,128)(2,1)} %get-tuple-element.41), channel_id=1, source_target_pairs={{0,5},{1,4},{2,7},{3,6},{4,1},{5,0},{6,3},{7,2},{8,13},{9,12},{10,... | collective-permute-start | bytes 4128776 | tf_op jit(solution)/shard_map/ppermute | solution.py:84
  187.6 448.5 %copy-start = (bf16[28,96,256]{2,1,0:T(8,128)(2,1)}, bf16[28,96,256]{2,1,0:T(8,128)(2,1)S(1)}, u32[]{:S(2)}) copy-start(bf16[28,96,256]{2,1,0:T(8,128)(2,1)S(1)} %collective-permute-done.refs_1_) | copy-start | bytes 4128772
  187.6 149.6 %collective-permute-start.5 = (bf16[28,96,256]{2,1,0:T(8,128)(2,1)}, bf16[28,96,256]{2,1,0:T(8,128)(2,1)}, u32[]{:S(2)}, u32[]{:S(2)}) collective-permute-start(bf16[28,96,256]{2,1,0:T(8,128)(2,1)} %get-tuple-element.42), channel_id=1, source_target_pairs={{0,6},{1,7},{2,4},{3,5},{4,2},{5,3},{6,0},{7,1},{8,14},{9,15},{10,... | collective-permute-start | bytes 4128776 | tf_op jit(solution)/shard_map/ppermute | solution.py:84
  188.6 447.6 %copy-start.1 = (bf16[28,96,256]{2,1,0:T(8,128)(2,1)}, bf16[28,96,256]{2,1,0:T(8,128)(2,1)S(1)}, u32[]{:S(2)}) copy-start(bf16[28,96,256]{2,1,0:T(8,128)(2,1)S(1)} %collective-permute-done.1.refs_2_) | copy-start | bytes 4128772
  188.6 210.0 %collective-permute-start.6 = (bf16[28,96,256]{2,1,0:T(8,128)(2,1)}, bf16[28,96,256]{2,1,0:T(8,128)(2,1)}, u32[]{:S(2)}, u32[]{:S(2)}) collective-permute-start(bf16[28,96,256]{2,1,0:T(8,128)(2,1)} %get-tuple-element.43), channel_id=1, source_target_pairs={{0,7},{1,6},{2,5},{3,4},{4,3},{5,2},{6,1},{7,0},{8,15},{9,14},{10,... | collective-permute-start | bytes 4128776 | tf_op jit(solution)/shard_map/ppermute | solution.py:84
  189.6 209.0 %collective-permute-start.21 = (bf16[28,96,256]{2,1,0:T(8,128)(2,1)}, bf16[28,96,256]{2,1,0:T(8,128)(2,1)}, u32[]{:S(2)}, u32[]{:S(2)}) collective-permute-start(bf16[28,96,256]{2,1,0:T(8,128)(2,1)} %get-tuple-element.60), channel_id=1, source_target_pairs={{0,1},{1,0},{2,3},{3,2},{4,5},{5,4},{6,7},{7,6},{8,9},{9,8},{10,11... | collective-permute-start | bytes 4128776 | tf_op jit(solution)/shard_map/ppermute | solution.py:84
  190.3 208.2 %collective-permute-start.22 = (bf16[28,96,256]{2,1,0:T(8,128)(2,1)}, bf16[28,96,256]{2,1,0:T(8,128)(2,1)}, u32[]{:S(2)}, u32[]{:S(2)}) collective-permute-start(bf16[28,96,256]{2,1,0:T(8,128)(2,1)} %get-tuple-element.61), channel_id=1, source_target_pairs={{0,2},{1,3},{2,0},{3,1},{4,6},{5,7},{6,4},{7,5},{8,10},{9,11},{10,... | collective-permute-start | bytes 4128776 | tf_op jit(solution)/shard_map/ppermute | solution.py:84
  304.8 96.8 %collective-permute-start.23 = (bf16[28,96,256]{2,1,0:T(8,128)(2,1)}, bf16[28,96,256]{2,1,0:T(8,128)(2,1)}, u32[]{:S(2)}, u32[]{:S(2)}) collective-permute-start(bf16[28,96,256]{2,1,0:T(8,128)(2,1)} %get-tuple-element.62), channel_id=1, source_target_pairs={{0,3},{1,2},{2,1},{3,0},{4,7},{5,6},{6,5},{7,4},{8,11},{9,10},{10,... | collective-permute-start | bytes 4128776 | tf_op jit(solution)/shard_map/ppermute | solution.py:84
  337.2 175.5 %collective-permute-start.24 = (bf16[28,96,256]{2,1,0:T(8,128)(2,1)}, bf16[28,96,256]{2,1,0:T(8,128)(2,1)}, u32[]{:S(2)}, u32[]{:S(2)}) collective-permute-start(bf16[28,96,256]{2,1,0:T(8,128)(2,1)} %get-tuple-element.63), channel_id=1, source_target_pairs={{0,4},{1,5},{2,6},{3,7},{4,0},{5,1},{6,2},{7,3},{8,12},{9,13},{10,... | collective-permute-start | bytes 4128776 | tf_op jit(solution)/shard_map/ppermute | solution.py:84
  398.5 147.9 %collective-permute-start.25 = (bf16[28,96,256]{2,1,0:T(8,128)(2,1)}, bf16[28,96,256]{2,1,0:T(8,128)(2,1)}, u32[]{:S(2)}, u32[]{:S(2)}) collective-permute-start(bf16[28,96,256]{2,1,0:T(8,128)(2,1)} %get-tuple-element.64), channel_id=1, source_target_pairs={{0,5},{1,4},{2,7},{3,6},{4,1},{5,0},{6,3},{7,2},{8,13},{9,12},{10,... | collective-permute-start | bytes 4128776 | tf_op jit(solution)/shard_map/ppermute | solution.py:84
  398.5 192.9 %collective-permute-start.26 = (bf16[28,96,256]{2,1,0:T(8,128)(2,1)}, bf16[28,96,256]{2,1,0:T(8,128)(2,1)}, u32[]{:S(2)}, u32[]{:S(2)}) collective-permute-start(bf16[28,96,256]{2,1,0:T(8,128)(2,1)} %get-tuple-element.65), channel_id=1, source_target_pairs={{0,6},{1,7},{2,4},{3,5},{4,2},{5,3},{6,0},{7,1},{8,14},{9,15},{10,... | collective-permute-start | bytes 4128776 | tf_op jit(solution)/shard_map/ppermute | solution.py:84
  398.5 223.3 %collective-permute-start.27 = (bf16[28,96,256]{2,1,0:T(8,128)(2,1)}, bf16[28,96,256]{2,1,0:T(8,128)(2,1)}, u32[]{:S(2)}, u32[]{:S(2)}) collective-permute-start(bf16[28,96,256]{2,1,0:T(8,128)(2,1)} %get-tuple-element.66), channel_id=1, source_target_pairs={{0,7},{1,6},{2,5},{3,4},{4,3},{5,2},{6,1},{7,0},{8,15},{9,14},{10,... | collective-permute-start | bytes 4128776 | tf_op jit(solution)/shard_map/ppermute | solution.py:84
  401.5 256.8 %collective-permute-start.16 = (bf16[4,96,256]{2,1,0:T(8,128)(2,1)}, bf16[4,96,256]{2,1,0:T(8,128)(2,1)}, u32[]{:S(2)}, u32[]{:S(2)}) collective-permute-start(bf16[4,96,256]{2,1,0:T(8,128)(2,1)} %get-tuple-element.55), channel_id=1, source_target_pairs={{0,3},{1,2},{2,1},{3,0},{4,7},{5,6},{6,5},{7,4},{8,11},{9,10},{10,... | collective-permute-start | bytes 589832 | tf_op jit(solution)/shard_map/ppermute | solution.py:84
  512.7 145.6 %collective-permute-start.17 = (bf16[4,96,256]{2,1,0:T(8,128)(2,1)}, bf16[4,96,256]{2,1,0:T(8,128)(2,1)}, u32[]{:S(2)}, u32[]{:S(2)}) collective-permute-start(bf16[4,96,256]{2,1,0:T(8,128)(2,1)} %get-tuple-element.56), channel_id=1, source_target_pairs={{0,4},{1,5},{2,6},{3,7},{4,0},{5,1},{6,2},{7,3},{8,12},{9,13},{10,... | collective-permute-start | bytes 589832 | tf_op jit(solution)/shard_map/ppermute | solution.py:84
  546.4 111.9 %collective-permute-start.18 = (bf16[4,96,256]{2,1,0:T(8,128)(2,1)}, bf16[4,96,256]{2,1,0:T(8,128)(2,1)}, u32[]{:S(2)}, u32[]{:S(2)}) collective-permute-start(bf16[4,96,256]{2,1,0:T(8,128)(2,1)} %get-tuple-element.57), channel_id=1, source_target_pairs={{0,5},{1,4},{2,7},{3,6},{4,1},{5,0},{6,3},{7,2},{8,13},{9,12},{10,... | collective-permute-start | bytes 589832 | tf_op jit(solution)/shard_map/ppermute | solution.py:84
  591.5 66.9 %collective-permute-start.19 = (bf16[4,96,256]{2,1,0:T(8,128)(2,1)}, bf16[4,96,256]{2,1,0:T(8,128)(2,1)}, u32[]{:S(2)}, u32[]{:S(2)}) collective-permute-start(bf16[4,96,256]{2,1,0:T(8,128)(2,1)} %get-tuple-element.58), channel_id=1, source_target_pairs={{0,6},{1,7},{2,4},{3,5},{4,2},{5,3},{6,0},{7,1},{8,14},{9,15},{10,... | collective-permute-start | bytes 589832 | tf_op jit(solution)/shard_map/ppermute | solution.py:84
  621.8 36.5 %collective-permute-start.20 = (bf16[4,96,256]{2,1,0:T(8,128)(2,1)}, bf16[4,96,256]{2,1,0:T(8,128)(2,1)}, u32[]{:S(2)}, u32[]{:S(2)}) collective-permute-start(bf16[4,96,256]{2,1,0:T(8,128)(2,1)} %get-tuple-element.59), channel_id=1, source_target_pairs={{0,7},{1,6},{2,5},{3,4},{4,3},{5,2},{6,1},{7,0},{8,15},{9,14},{10,... | collective-permute-start | bytes 589832 | tf_op jit(solution)/shard_map/ppermute | solution.py:84
  (9 other events, 131.5 us)
